TPU v7x, 128 devices: a whole 4x4x4 slice. The times are simulated.
128 devices in a mesh: ctx: 16 (over x, z), tp: 8 (over y, core).
Axes of the slice: x: 4, y: 4, z: 4, core: 2. Of those that a mesh axis runs over, the one named last changes fastest.
Arguments:
- queries: bfloat16 [512, 8192], P('ctx', 'tp'), may hold values from -6 to 6
- cache_keys: bfloat16 [65536, 1024], P('ctx', 'tp'), may hold values from -18 to 18
- cache_values: bfloat16 [65536, 1024], P('ctx', 'tp'), may hold values from -6 to 6
- span_keys: bfloat16 [512, 1024], P('ctx', 'tp'), may hold values from -24 to 24
- span_values: bfloat16 [512, 1024], P('ctx', 'tp'), may hold values from -6 to 6
- out_weight: bfloat16 [8192, 8192], P('tp', 'ctx'), may hold values from -0.0625 to 0.0625
- residual: bfloat16 [512, 8192], P('tp', 'ctx'), may hold values from -72 to 72
- norm_gain: bfloat16 [8192], P('ctx'), may hold values from 0.5 to 1.5
- head_weight: bfloat16 [8192, 128256], P(None, ('ctx', 'tp')), may hold values from -0.198873782 to 0.198873782
- targets: int32 [512], replicated, may hold values from 0 to 128255
- window_lengths: int32 [8], replicated, may hold values from 1 to 128, 512 in all
Outputs:
- token_logprob: float32 [512], P('ctx')
- window_means: float32 [8], replicated
Inputs may be any that keep to these rules, and one draw needn't show every extreme that they name: `window_lengths`: the 8 lengths sum to 512.
All inputs are finite; a program needn't handle non-finite values.
Results may differ from a plain program's by a relative error of at most 0.0025.
Values may be sent and summed in bfloat16 or wider, within the bound.
No kernel may reach another device: no remote copies, remote signals or barrier semaphores. Data moves between devices by JAX's collectives and lax.ppermute only.
A program may use at most 128 MiB of HBM per device.

v0:
```python
import jax
import jax.numpy as jnp
from jax import lax
from jax.sharding import Mesh
from jax.sharding import PartitionSpec as P

D = 8192
HEADS = 64
KV_HEADS = 8
HD = 128
CTX = ("ctx_0", "ctx_1")
TP = ("tp_0", "tp_1")
CTX_TP = ("ctx_0", "ctx_1", "tp_0", "tp_1")
EPSILON = 1e-05
NEGATIVE = -1e30


def in_order(blocks, dim):
    blocks = jnp.moveaxis(blocks, 0, dim)
    shape = blocks.shape
    return blocks.reshape(*shape[:dim], shape[dim] * shape[dim + 1], *shape[dim + 2 :])


def sent_to_all(value, axis):
    count = lax.axis_size(axis)
    return lax.all_to_all(
        jnp.broadcast_to(value[None], (count, *value.shape)), axis, 0, 0, tiled=True
    )


def gathered_copies(value, axis, dim):
    return in_order(sent_to_all(value, axis), dim)


def sent_together(arrays, axis, split_dim, concat_dim, along):
    ends, at = ([], 0)
    for a in arrays[:-1]:
        at += a.shape[along]
        ends.append(at)
    both = jnp.concatenate(arrays, axis=along)
    return tuple(
        jnp.split(
            lax.all_to_all(both, axis, split_axis=split_dim, concat_axis=concat_dim, tiled=True),
            ends,
            axis=along,
        )
    )


def in_blocks(value, dim, count):
    shape = value.shape
    blocks = value.reshape(*shape[:dim], count, shape[dim] // count, *shape[dim + 1 :])
    return jnp.moveaxis(blocks, dim, 0)


def summed_on_arrival(value, axis, dim):
    blocks = in_blocks(value, dim, lax.axis_size(axis))
    arrived = lax.all_to_all(blocks, axis, split_axis=0, concat_axis=0, tiled=True)
    return arrived.astype(jnp.float32).sum(axis=0)


def over_axes(value, axes):
    for axis in axes:
        value = lax.psum(value, axis)
    return value


def gathered_once(value, axis):
    leaves = jax.tree.leaves(value)
    order = sorted(range(len(leaves)), key=lambda k: -leaves[k].size)
    width = (1, *leaves[order[0]].shape)[-1]
    lines = [
        jnp.pad(leaves[k].reshape(-1), (0, -leaves[k].size % width)).reshape(-1, width)
        for k in order
    ]
    both, at, found = (lax.all_gather(jnp.concatenate(lines), axis), 0, {})
    for k, line in zip(order, lines):
        slab = both[:, at : at + len(line)].reshape(len(both), -1)
        found[k] = slab[:, : leaves[k].size].reshape(-1, *leaves[k].shape)
        at += len(line)
    numbers = iter(range(len(leaves)))
    return jax.tree.map(lambda _: found[next(numbers)], value)


def combined_by_axis(value, axes, combine):
    for axis in axes:
        pieces = gathered_once(value, axis)
        value = jax.tree.map(lambda part: part[0], pieces)
        for k in range(1, lax.axis_size(axis)):
            value = combine(value, jax.tree.map(lambda part: part[k], pieces))
    return value


def fold_block(state, scores, value_rows):
    row_max, row_sum, weighted = state
    new_max = jnp.maximum(row_max, jnp.max(scores, axis=1))
    fading = jnp.exp(row_max - new_max)
    weights = jnp.exp(scores - new_max[:, None])
    row_sum = row_sum * fading + jnp.sum(weights, axis=1)
    weighted = weighted * fading[:, None] + jnp.dot(
        weights.astype(jnp.bfloat16), value_rows, preferred_element_type=jnp.float32
    )
    return (new_max, row_sum, weighted)


def partial_head(
    query_rows, cache_part, value_part, fresh_keys, fresh_values, first_token, span_total
):
    row_count = query_rows.shape[0]
    scaling = HD ** (-0.5)
    block_size = min(1024, cache_part.shape[0])
    block_count = cache_part.shape[0] // block_size
    key_blocks = cache_part.reshape(block_count, block_size, HD)
    value_blocks = value_part.reshape(block_count, block_size, HD)

    def advance(state, block_pair):
        scores = jnp.dot(query_rows, block_pair[0].T, preferred_element_type=jnp.float32) * scaling
        return (fold_block(state, scores, block_pair[1]), None)

    start_state = (
        jnp.full((row_count,), NEGATIVE, jnp.float32),
        jnp.zeros((row_count,), jnp.float32),
        jnp.zeros((row_count, HD), jnp.float32),
    )
    state, unused = lax.scan(advance, start_state, (key_blocks, value_blocks))
    scores = jnp.dot(query_rows, fresh_keys.T, preferred_element_type=jnp.float32) * scaling
    token_of_row = jnp.arange(row_count, dtype=jnp.int32) % span_total
    key_token = first_token + jnp.arange(fresh_keys.shape[0], dtype=jnp.int32)
    scores = jnp.where(token_of_row[:, None] >= key_token[None, :], scores, NEGATIVE)
    return fold_block(state, scores, fresh_values)


def combine_logits(first, second):
    row_max = jnp.maximum(first[0], second[0])
    row_sum = first[1] * jnp.exp(first[0] - row_max) + second[1] * jnp.exp(second[0] - row_max)
    return (row_max, row_sum, first[2] + second[2])


def local(
    queries,
    cache_keys,
    cache_values,
    span_keys,
    span_values,
    out_weight,
    residual,
    norm_gain,
    head_weight,
    targets,
    window_lengths,
):
    ctx_rank = lax.axis_index(CTX)
    span_dev = queries.shape[0]
    group_size = HEADS // KV_HEADS
    kv_local = cache_keys.shape[1] // HD
    heads_local = kv_local * group_size
    query_all = gathered_copies(queries, CTX, 0)
    span_total = query_all.shape[0]
    query_heads = (
        query_all.reshape(span_total, kv_local, group_size, HD)
        .transpose(1, 2, 0, 3)
        .reshape(kv_local, group_size * span_total, HD)
    )
    first_token = ctx_rank * span_dev
    row_max, row_sum, weighted = partial_head(
        query_heads[0], cache_keys, cache_values, span_keys, span_values, first_token, span_total
    )
    maxima = [row_max]
    totals = [row_sum]
    weighted_rows = [weighted]
    part_max = (
        jnp.stack(maxima)
        .reshape(kv_local, group_size, span_total)
        .transpose(2, 0, 1)
        .reshape(span_total, heads_local)
    )
    part_sum = (
        jnp.stack(totals)
        .reshape(kv_local, group_size, span_total)
        .transpose(2, 0, 1)
        .reshape(span_total, heads_local)
    )
    part_weighted = (
        jnp.stack(weighted_rows)
        .reshape(kv_local, group_size, span_total, HD)
        .transpose(2, 0, 1, 3)
        .reshape(span_total, heads_local * HD)
    )
    pieces = tuple(
        (
            part.astype(jnp.float32)
            for part in sent_together(
                (
                    part_max[None].astype(jnp.bfloat16),
                    part_sum[None].astype(jnp.bfloat16),
                    part_weighted[None].astype(jnp.bfloat16),
                ),
                CTX,
                1,
                0,
                2,
            )
        )
    )
    source_count = pieces[0].shape[0]
    row_max = jnp.max(pieces[0], axis=0)
    fading = jnp.exp(pieces[0] - row_max[None])
    row_sum = jnp.sum(pieces[1] * fading, axis=0)
    weighted = jnp.sum(
        pieces[2].reshape(source_count, span_dev, heads_local, HD) * fading[:, :, :, None], axis=0
    )
    attended_own = (
        (weighted / row_sum[:, :, None]).reshape(span_dev, heads_local * HD).astype(jnp.bfloat16)
    )
    attended_all = gathered_copies(attended_own, CTX, 0)
    projected = summed_on_arrival(
        jnp.dot(attended_all, out_weight, preferred_element_type=jnp.float32).astype(jnp.bfloat16),
        TP,
        0,
    )
    stream = residual.astype(jnp.float32) + projected
    squares = over_axes(jnp.sum(stream * stream, axis=1), CTX)
    scaled = lax.rsqrt(squares / D + EPSILON)
    normed_part = (stream * scaled[:, None] * norm_gain.astype(jnp.float32)[None, :]).astype(
        jnp.bfloat16
    )
    normed_rows = gathered_copies(normed_part, CTX, 1)
    logits = jnp.dot(
        lax.all_gather(normed_rows, TP, axis=0, tiled=True),
        head_weight,
        preferred_element_type=jnp.float32,
    )
    vocab_dev = head_weight.shape[1]
    vocab_start = lax.axis_index(CTX_TP) * vocab_dev
    columns = vocab_start + jnp.arange(vocab_dev, dtype=jnp.int32)
    target_part = jnp.sum(jnp.where(targets[:, None] == columns[None, :], logits, 0.0), axis=1)
    local_max = jnp.max(logits, axis=1)
    exp_part = jnp.sum(jnp.exp(logits - local_max[:, None]), axis=1)
    global_max, exp_total, target_logit = combined_by_axis(
        (local_max, exp_part, target_part), CTX_TP, combine_logits
    )
    token_logprob = target_logit - (global_max + jnp.log(exp_total))
    window_ends = jnp.cumsum(window_lengths)
    window_starts = window_ends - window_lengths
    positions = jnp.arange(span_total, dtype=jnp.int32)
    member = (
        (positions[None, :] >= window_starts[:, None]) & (positions[None, :] < window_ends[:, None])
    ).astype(jnp.float32)
    window_sums = jnp.dot(member, token_logprob)
    window_means = window_sums / window_lengths.astype(jnp.float32)
    own_logprob = lax.dynamic_slice_in_dim(token_logprob, first_token, span_dev, 0)
    return (own_logprob, window_means)


def solution(mesh):
    split = Mesh(mesh.devices.reshape(4, 4, 4, 2), ("ctx_0", "ctx_1", "tp_0", "tp_1"))
    in_specs = (
        P(CTX, TP),
        P(CTX, TP),
        P(CTX, TP),
        P(CTX, TP),
        P(CTX, TP),
        P(TP, CTX),
        P(TP, CTX),
        P(CTX),
        P(None, CTX_TP),
        P(),
        P(),
    )
    out_specs = (P(CTX), P())
    return jax.shard_map(local, mesh=split, in_specs=in_specs, out_specs=out_specs, check_vma=False)
```

profile of v0, /device:TPU:1, one launch (start us, length us, event | category | flops | bytes accessed | tf_op | source)
XLA Modules:
  0.0 373.4 jit_solution(12038084039484746735)
XLA Ops:
  7.2 0.0 copy-start
  7.2 2.1 broadcast_in_dim.24
  9.3 8.5 %all-to-all-start = ((bf16[16,32,1024]{2,1,0:T(8,128)(2,1)}), bf16[16,32,1024]{2,1,0:T(8,128)(2,1)}, u32[]{:S(2)}, u32[]{:S(2)}) async-start(bf16[16,32,1024]{2,1,0:T(8,128)(2,1)} %broadcast_in_dim.24), calls=%async_computation | async-start | bytes 2097152 | tf_op jit(solution)/shard_map/all_to_all | solution.py:26
  17.8 15.7 %all-to-all-done = bf16[16,32,1024]{2,1,0:T(8,128)(2,1)} async-done(((bf16[16,32,1024]{2,1,0:T(8,128)(2,1)}), bf16[16,32,1024]{2,1,0:T(8,128)(2,1)}, u32[]{:S(2)}, u32[]{:S(2)}) %all-to-all-start) | async-done | bytes 1048608 | tf_op jit(solution)/shard_map/all_to_all | solution.py:26
  33.5 1.5 copy.25
  35.0 1.2 copy.19
  36.1 102.5 %while.15 = (s32[]{:T(128)}, f32[4096]{0:T(1024)S(1)}, f32[4096]{0:T(1024)S(1)}, f32[4096,128]{1,0:T(8,128)S(1)}, bf16[4,1024,128]{2,1,0:T(8,128)(2,1)}, /*index...) while((s32[]{:T(128)}, f32[4096]{0:T(1024)S(1)}, ...), condition=%wide.region_3.4_spmd.clone, body=%wide.region_0.3_spmd.clone.sunk | while | flops 2182631424 | bytes 56361076 | solution.py:125
  36.1 9.4 %multiply_reduce_fusion.5 = (f32[4096]{0:T(1024)S(1)}, f32[1024,4096]{1,0:T(8,128)}) fusion(bf16[4096,128]{1,0:T(8,128)(2,1)} %get-tuple-element.183, bf16[4,1024,128]{2,1,0:T(8,128)(2,1)} %get-tuple-element.182, s32[]{:T(128)S(6)} %copy.32), kind=kOutput, calls=%fused_computation.1.clone.1 | convolution fusion | flops 1082126336 | bytes 18104324 | tf_op jit(solution)/shard_map/while/body/eval_jaxpr/dot_general | solution.py:117
  45.5 8.5 %fusion.99 = f32[4096]{0:T(1024)S(1)} fusion(f32[1024,4096]{1,0:T(8,128)} %get-tuple-element.157, f32[4096]{0:T(1024)S(1)} %select_maximum_fusion.2), kind=kLoop, calls=%fused_computation.3.clone.1 | loop fusion | flops 12578816 | bytes 16809984 | tf_op jit(solution)/shard_map/while/body/eval_jaxpr/reduce_sum | solution.py:99
  54.1 7.7 %fusion.101 = f32[4096,128]{1,0:T(8,128)S(1)} fusion(f32[1024,4096]{1,0:T(8,128)} %get-tuple-element.157, f32[4096]{0:T(1024)S(1)} %select_maximum_fusion.2, f32[4096,128]{1,0:T(8,128)S(1)} %get-tuple-element.172, f32[4096]{0:T(1024)S(1)} %get-tuple-element.159, pred[]{:T(512)S(6)} %compare.4, bf16[4,1024,128]{2,1,0:T(8,128)(2,1)} %get-tuple-element.184, ...), kind=kOutput, calls=%fused_computation.7.clone.1 | convolution fusion | flops 1087897600 | bytes 21266436 | tf_op jit(solution)/shard_map/while/body/eval_jaxpr/dot_general | solution.py:100
  61.8 9.4 %multiply_reduce_fusion.5 = (f32[4096]{0:T(1024)S(1)}, f32[1024,4096]{1,0:T(8,128)}) fusion(bf16[4096,128]{1,0:T(8,128)(2,1)} %get-tuple-element.183, bf16[4,1024,128]{2,1,0:T(8,128)(2,1)} %get-tuple-element.182, s32[]{:T(128)S(6)} %copy.32), kind=kOutput, calls=%fused_computation.1.clone.1 | convolution fusion | flops 1082126336 | bytes 18104324 | tf_op jit(solution)/shard_map/while/body/eval_jaxpr/dot_general | solution.py:117
  71.1 8.5 %fusion.99 = f32[4096]{0:T(1024)S(1)} fusion(f32[1024,4096]{1,0:T(8,128)} %get-tuple-element.157, f32[4096]{0:T(1024)S(1)} %select_maximum_fusion.2), kind=kLoop, calls=%fused_computation.3.clone.1 | loop fusion | flops 12578816 | bytes 16809984 | tf_op jit(solution)/shard_map/while/body/eval_jaxpr/reduce_sum | solution.py:99
  79.7 7.7 %fusion.101 = f32[4096,128]{1,0:T(8,128)S(1)} fusion(f32[1024,4096]{1,0:T(8,128)} %get-tuple-element.157, f32[4096]{0:T(1024)S(1)} %select_maximum_fusion.2, f32[4096,128]{1,0:T(8,128)S(1)} %get-tuple-element.172, f32[4096]{0:T(1024)S(1)} %get-tuple-element.159, pred[]{:T(512)S(6)} %compare.4, bf16[4,1024,128]{2,1,0:T(8,128)(2,1)} %get-tuple-element.184, ...), kind=kOutput, calls=%fused_computation.7.clone.1 | convolution fusion | flops 1087897600 | bytes 21266436 | tf_op jit(solution)/shard_map/while/body/eval_jaxpr/dot_general | solution.py:100
  87.4 9.4 %multiply_reduce_fusion.5 = (f32[4096]{0:T(1024)S(1)}, f32[1024,4096]{1,0:T(8,128)}) fusion(bf16[4096,128]{1,0:T(8,128)(2,1)} %get-tuple-element.183, bf16[4,1024,128]{2,1,0:T(8,128)(2,1)} %get-tuple-element.182, s32[]{:T(128)S(6)} %copy.32), kind=kOutput, calls=%fused_computation.1.clone.1 | convolution fusion | flops 1082126336 | bytes 18104324 | tf_op jit(solution)/shard_map/while/body/eval_jaxpr/dot_general | solution.py:117
  96.8 8.5 %fusion.99 = f32[4096]{0:T(1024)S(1)} fusion(f32[1024,4096]{1,0:T(8,128)} %get-tuple-element.157, f32[4096]{0:T(1024)S(1)} %select_maximum_fusion.2), kind=kLoop, calls=%fused_computation.3.clone.1 | loop fusion | flops 12578816 | bytes 16809984 | tf_op jit(solution)/shard_map/while/body/eval_jaxpr/reduce_sum | solution.py:99
  105.3 7.7 %fusion.101 = f32[4096,128]{1,0:T(8,128)S(1)} fusion(f32[1024,4096]{1,0:T(8,128)} %get-tuple-element.157, f32[4096]{0:T(1024)S(1)} %select_maximum_fusion.2, f32[4096,128]{1,0:T(8,128)S(1)} %get-tuple-element.172, f32[4096]{0:T(1024)S(1)} %get-tuple-element.159, pred[]{:T(512)S(6)} %compare.4, bf16[4,1024,128]{2,1,0:T(8,128)(2,1)} %get-tuple-element.184, ...), kind=kOutput, calls=%fused_computation.7.clone.1 | convolution fusion | flops 1087897600 | bytes 21266436 | tf_op jit(solution)/shard_map/while/body/eval_jaxpr/dot_general | solution.py:100
  113.0 9.4 %multiply_reduce_fusion.5 = (f32[4096]{0:T(1024)S(1)}, f32[1024,4096]{1,0:T(8,128)}) fusion(bf16[4096,128]{1,0:T(8,128)(2,1)} %get-tuple-element.183, bf16[4,1024,128]{2,1,0:T(8,128)(2,1)} %get-tuple-element.182, s32[]{:T(128)S(6)} %copy.32), kind=kOutput, calls=%fused_computation.1.clone.1 | convolution fusion | flops 1082126336 | bytes 18104324 | tf_op jit(solution)/shard_map/while/body/eval_jaxpr/dot_general | solution.py:117
  122.4 8.5 %fusion.99 = f32[4096]{0:T(1024)S(1)} fusion(f32[1024,4096]{1,0:T(8,128)} %get-tuple-element.157, f32[4096]{0:T(1024)S(1)} %select_maximum_fusion.2), kind=kLoop, calls=%fused_computation.3.clone.1 | loop fusion | flops 12578816 | bytes 16809984 | tf_op jit(solution)/shard_map/while/body/eval_jaxpr/reduce_sum | solution.py:99
  131.0 7.7 %fusion.101 = f32[4096,128]{1,0:T(8,128)S(1)} fusion(f32[1024,4096]{1,0:T(8,128)} %get-tuple-element.157, f32[4096]{0:T(1024)S(1)} %select_maximum_fusion.2, f32[4096,128]{1,0:T(8,128)S(1)} %get-tuple-element.172, f32[4096]{0:T(1024)S(1)} %get-tuple-element.159, pred[]{:T(512)S(6)} %compare.4, bf16[4,1024,128]{2,1,0:T(8,128)(2,1)} %get-tuple-element.184, ...), kind=kOutput, calls=%fused_computation.7.clone.1 | convolution fusion | flops 1087897600 | bytes 21266436 | tf_op jit(solution)/shard_map/while/body/eval_jaxpr/dot_general | solution.py:100
  138.7 0.0 copy-start.4
  138.7 1.7 fusion.79
  140.4 0.1 fusion.22
  140.5 1.8 fusion.18
  142.4 1.5 copy.20
  143.9 1.1 pad_maximum_fusion
  145.0 5.2 %copy.21 = bf16[1,512,1040]{2,0,1:T(2,128)(2,1)S(1)} copy(bf16[1,512,1040]{1,2,0:T(8,128)(2,1)} %pad_maximum_fusion) | data formatting | bytes 2129920 | tf_op jit(solution)/shard_map/concatenate | solution.py:40
  150.2 0.5 broadcast.82
  150.8 9.2 %reduce.4 = bf16[512,1040]{1,0:T(8,128)(2,1)} reduce(bf16[512,1,1040]{2,1,0:T(2,128)(2,1)S(1)} %bitcast.306, bf16[]{:T(256)} %broadcast.82), dimensions={1}, to_apply=%bitcast.273.reduce_sub_computation | reduce | bytes 2129922
  159.9 3.9 %reshape.901 = bf16[16,2,16640]{2,1,0:T(2,128)(2,1)S(1)} reshape(bf16[512,1040]{1,0:T(8,128)(2,1)} %reduce.4) | data formatting | bytes 2129920
  163.8 18.9 %all_to_all.32 = bf16[16,2,16640]{2,1,0:T(2,128)(2,1)} all-to-all(bf16[16,2,16640]{2,1,0:T(2,128)(2,1)S(1)} %reshape.901), channel_id=1, replica_groups=mesh['ctx_0'=4,'ctx_1'=4,'tp_0'=4,'tp_1'=2] {'ctx_0','ctx_1'}, dimensions={0} | all-to-all | bytes 2129920 | tf_op jit(solution)/shard_map/all_to_all | solution.py:43
  182.7 4.8 %reshape.902 = bf16[512,1,1040]{2,1,0:T(2,128)(2,1)S(1)} reshape(bf16[16,2,16640]{2,1,0:T(2,128)(2,1)} %all_to_all.32) | data formatting | bytes 2129920
  187.6 0.2 copy.23
  187.8 0.1 multiply_reduce_fusion.2
  187.9 0.9 copy-done.1
  188.8 2.0 mul.276
  190.7 1.7 mul.277
  192.4 1.8 multiply_reduce_fusion.1
  194.2 0.1 div.24
  194.4 0.1 broadcast_in_dim.26
  194.5 16.1 %all_to_all.33 = bf16[16,32,1024]{2,1,0:T(8,128)(2,1)S(1)} all-to-all(bf16[16,32,1024]{2,1,0:T(8,128)(2,1)S(1)} %broadcast_in_dim.26), channel_id=1, replica_groups=mesh['ctx_0'=4,'ctx_1'=4,'tp_0'=4,'tp_1'=2] {'ctx_0','ctx_1'}, dimensions={0} | all-to-all | bytes 2097152 | tf_op jit(solution)/shard_map/all_to_all | solution.py:26
  210.6 1.5 convolution_convert_fusion
  212.1 9.2 %all-to-all-start.3 = ((bf16[8,64,512]{2,1,0:T(8,128)(2,1)}), bf16[8,64,512]{2,1,0:T(8,128)(2,1)S(1)}, u32[]{:S(2)}, u32[]{:S(2)}) async-start(bf16[8,64,512]{2,1,0:T(8,128)(2,1)} %bitcast.12), calls=%async_computation.3 | async-start | bytes 1048576 | tf_op jit(solution)/shard_map/all_to_all | solution.py:58
  221.3 0.0 all-gather.10.cloned.1.call-start
  221.3 9.3 %all-to-all-done.3 = bf16[8,64,512]{2,1,0:T(8,128)(2,1)S(1)} async-done(((bf16[8,64,512]{2,1,0:T(8,128)(2,1)}), bf16[8,64,512]{2,1,0:T(8,128)(2,1)S(1)}, u32[]{:S(2)}, u32[]{:S(2)}) %all-to-all-start.3) | async-done | bytes 524320 | tf_op jit(solution)/shard_map/all_to_all | solution.py:58
  230.6 0.1 convert_reduce_fusion
  230.7 0.0 copy-done.2
  230.7 0.1 multiply_reduce_fusion.3
  230.8 6.8 %psum.14 = f32[64]{0:T(128)S(1)} all-reduce(f32[64]{0:T(128)S(1)} %multiply_reduce_fusion.3), channel_id=1, replica_groups=mesh['ctx_0'=4,'ctx_1'=4,'tp_0'=4,'tp_1'=2] {'ctx_0'}, use_global_device_ids=true, to_apply=%region_11.12 | all-reduce | flops 64 | bytes 512 | tf_op jit(solution)/shard_map/psum | solution.py:64
  237.7 6.3 %psum.15 = f32[64]{0:T(128)S(1)} all-reduce(f32[64]{0:T(128)S(1)} %psum.14), channel_id=1, replica_groups=mesh['ctx_0'=4,'ctx_1'=4,'tp_0'=4,'tp_1'=2] {'ctx_1'}, use_global_device_ids=true, to_apply=%region_12.13 | all-reduce | flops 64 | bytes 512 | tf_op jit(solution)/shard_map/psum | solution.py:64
  244.0 0.1 multiply_convert_fusion
  244.1 0.1 broadcast_in_dim.27
  244.2 15.1 %all_to_all.34 = bf16[16,64,512]{2,1,0:T(8,128)(2,1)S(1)} all-to-all(bf16[16,64,512]{2,1,0:T(8,128)(2,1)S(1)} %broadcast_in_dim.27), channel_id=1, replica_groups=mesh['ctx_0'=4,'ctx_1'=4,'tp_0'=4,'tp_1'=2] {'ctx_0','ctx_1'}, dimensions={0} | all-to-all | bytes 2097152 | tf_op jit(solution)/shard_map/all_to_all | solution.py:26
  259.3 1.2 copy.24
  260.4 0.0 all-gather.10.cloned.1.call-update
  260.5 0.2 reduce-window.8
  260.7 51.3 %all-gather.10.cloned.1.call-done = bf16[512,8192]{1,0:T(8,128)(2,1)} async-done(((bf16[64,8192]{1,0:T(8,128)(2,1)}), bf16[512,8192]{1,0:T(8,128)(2,1)}) %all-gather.10.cloned.1.call-update) | async-done | bytes 8388624 | tf_op jit(solution)/shard_map/all_gather | solution.py:229
  312.0 14.2 %fusion.80 = (f32[512]{0:T(512)S(1)}, f32[512,1002]{0,1:T(8,128)S(1)}) fusion(bf16[512,8192]{1,0:T(8,128)(2,1)} %all-gather.10.cloned.1.call-done, bf16[8192,1002]{0,1:T(8,128)(2,1)} %param.21), kind=kOutput, calls=%fused_computation.145 | convolution fusion | flops 8405897728 | bytes 26859520 | tf_op jit(solution)/shard_map/dot_general | solution.py:228
  326.2 0.5 exponential_reduce_fusion
  326.7 9.6 %all-gather.4 = f32[4,3,512]{2,1,0:T(4,128)S(1)} all-gather(f32[1,3,512]{2,1,0:T(4,128)S(1)} %maximum_bitcast_fusion), channel_id=2, replica_groups=mesh['ctx_0'=4,'ctx_1'=4,'tp_0'=4,'tp_1'=2] {'ctx_0'}, dimensions={0}, use_global_device_ids=true | all-gather | bytes 30720 | tf_op jit(solution)/shard_map/all_gather | solution.py:76
  336.4 9.5 %all-gather.5 = f32[4,3,512]{2,1,0:T(4,128)S(1)} all-gather(f32[1,3,512]{2,1,0:T(4,128)S(1)} %maximum_bitcast_fusion.1), channel_id=3, replica_groups=mesh['ctx_0'=4,'ctx_1'=4,'tp_0'=4,'tp_1'=2] {'ctx_1'}, dimensions={0}, use_global_device_ids=true | all-gather | bytes 30720 | tf_op jit(solution)/shard_map/all_gather | solution.py:76
  346.0 9.0 %all-gather.6 = f32[4,3,512]{2,1,0:T(4,128)S(1)} all-gather(f32[1,3,512]{2,1,0:T(4,128)S(1)} %maximum_bitcast_fusion.2), channel_id=4, replica_groups=mesh['ctx_0'=4,'ctx_1'=4,'tp_0'=4,'tp_1'=2] {'tp_0'}, dimensions={0}, use_global_device_ids=true | all-gather | bytes 30720 | tf_op jit(solution)/shard_map/all_gather | solution.py:76
  355.1 10.1 %all-gather.7 = f32[2,3,512]{2,1,0:T(4,128)S(1)} all-gather(f32[1,3,512]{2,1,0:T(4,128)S(1)} %maximum_bitcast_fusion.3), channel_id=5, replica_groups=mesh['ctx_0'=4,'ctx_1'=4,'tp_0'=4,'tp_1'=2] {'tp_1'}, dimensions={0}, use_global_device_ids=true | all-gather | bytes 18432 | tf_op jit(solution)/shard_map/all_gather | solution.py:76
  365.3 0.6 dynamic_slice.10
  365.8 0.7 fusion.20
  (52 shorter events, 0.5 us)
Async XLA Ops:
  7.2 203.5 %copy-start = (bf16[1024,512]{1,0:T(8,128)(2,1)S(1)}, bf16[1024,512]{1,0:T(8,128)(2,1)}, u32[]{:S(2)}) copy-start(bf16[1024,512]{1,0:T(8,128)(2,1)} %param.18) | copy-start | bytes 3145732
  9.3 24.2 %all-to-all-start = ((bf16[16,32,1024]{2,1,0:T(8,128)(2,1)}), bf16[16,32,1024]{2,1,0:T(8,128)(2,1)}, u32[]{:S(2)}, u32[]{:S(2)}) async-start(bf16[16,32,1024]{2,1,0:T(8,128)(2,1)} %broadcast_in_dim.24), calls=%async_computation | async-start | bytes 2097152 | tf_op jit(solution)/shard_map/all_to_all | solution.py:26
  36.1 102.5 %copy-start.3 = (bf16[32,128]{1,0:T(8,128)(2,1)S(1)}, bf16[32,128]{1,0:T(8,128)(2,1)}, u32[]{:S(2)}) copy-start(bf16[32,128]{1,0:T(8,128)(2,1)} %param.16) | copy-start | bytes 24580
  138.7 1.9 copy-start.4
  187.7 1.0 copy-start.1
  210.6 10.7 %copy-start.6 = (bf16[512]{0:T(512)(128)(2,1)S(1)}, bf16[512]{0:T(512)(128)(2,1)}, u32[]{:S(2)}) copy-start(bf16[512]{0:T(512)(128)(2,1)} %param.20) | copy-start | bytes 3076
  210.6 20.1 %copy-start.2 = (bf16[64,512]{1,0:T(8,128)(2,1)S(1)}, bf16[64,512]{1,0:T(8,128)(2,1)}, u32[]{:S(2)}) copy-start(bf16[64,512]{1,0:T(8,128)(2,1)} %param.19) | copy-start | bytes 196612
  212.1 18.5 %all-to-all-start.3 = ((bf16[8,64,512]{2,1,0:T(8,128)(2,1)}), bf16[8,64,512]{2,1,0:T(8,128)(2,1)S(1)}, u32[]{:S(2)}, u32[]{:S(2)}) async-start(bf16[8,64,512]{2,1,0:T(8,128)(2,1)} %bitcast.12), calls=%async_computation.3 | async-start | bytes 1048576 | tf_op jit(solution)/shard_map/all_to_all | solution.py:58
  221.3 90.7 %all-gather.10.cloned.1.call-start = ((), (), s32[]{:S(2)}) async-start(), calls=%async_computation.5 | async-start | bytes 9437184 | tf_op jit(solution)/shard_map/all_gather | solution.py:229
  259.3 1.2 copy-start.7
  260.7 65.5 %copy-start.5 = (s32[512]{0:T(512)S(1)}, s32[512]{0:T(512)}, u32[]{:S(2)}) copy-start(s32[512]{0:T(512)} %param.22) | copy-start | bytes 6148
Sparse Core Ops, SparseCore 0:
  260.6 51.3 all-gather.9
where the time goes:
time: 374 us; the launch traced here: 373 us
  blocking collectives  102 us (27%)
  matrix products  88.1 us (24%)
  waiting for transfers between devices  76.3 us (20%)
  other arithmetic  47.7 us (13%)
  local copies, waits for them, and re-layouts  27.5 us (7%)
  starting transfers between devices  17.6 us (5%)
  between operations  14.4 us (4%)
    all_gather x1, waiting for transfers between devices, local(): lax.all_gather(normed_rows, TP, axis=0, tiled=True)  51.3 us
    all_gather x4, blocking collectives, gathered_once(): both, at, found = (lax.all_gather(jnp.concatenate(lines), axis), 0, {})  38.3 us
    dot_general x4, matrix products, advance(): jnp.dot(query_rows, block_pair[0].T, preferred_element_type=jnp.float32)  37.5 us
    reduce_sum x5, other arithmetic, fold_block(): row_sum = row_sum * fading + jnp.sum(weights, axis=1)  34.2 us
    dot_general x5, matrix products, fold_block(): jnp.dot(weights.astype(jnp.bfloat16), value_rows, preferred_element_type=...  32.5 us
    all_to_all x2, blocking collectives, sent_to_all(): lax.all_to_all(jnp.broadcast_to(value[None], (count, *value.shape)), axis...  31.2 us
    all_to_all x1, blocking collectives, sent_together(): lax.all_to_all(both, axis, split_axis=split_dim, concat_axis=concat_dim,...  18.9 us
    all_to_all x1, waiting for transfers between devices, sent_to_all(): lax.all_to_all(jnp.broadcast_to(value[None], (count, *value.shape)), axis...  15.7 us
  transfers between devices with their start and end apart: 3, of which 3 were waited for; matrix products, arithmetic and copies ran while one was open for 0% of the time, Pallas kernels for 0%

commit v1 on v0

--- a/solution.py
+++ b/solution.py
@@ -225,11 +225,14 @@
         jnp.bfloat16
     )
     normed_rows = gathered_copies(normed_part, CTX, 1)
-    logits = jnp.dot(
-        lax.all_gather(normed_rows, TP, axis=0, tiled=True),
-        head_weight,
-        preferred_element_type=jnp.float32,
-    )
+
+    def ports_arrange(point, array_dim):
+        m_next = tuple((point for _ in range(lax.psum(1, TP))))
+        view_out = jnp.stack(m_next)
+        res = lax.all_to_all(view_out, TP, 0, 0)
+        return jnp.concatenate(res, axis=array_dim)
+
+    logits = jnp.dot(ports_arrange(normed_rows, 0), head_weight, preferred_element_type=jnp.float32)
     vocab_dev = head_weight.shape[1]
     vocab_start = lax.axis_index(CTX_TP) * vocab_dev
     columns = vocab_start + jnp.arange(vocab_dev, dtype=jnp.int32)

time: 374 us -> 417 us (1.11)
  waiting for transfers between devices: 76.3 us -> 119 us
  between operations: 14.4 us -> 1 us
  starting transfers between devices: 17.6 us -> 28.6 us
    all_to_all x0 -> x1, waiting for transfers between devices: none -> 93.6 us  [ports_arrange(): res = lax.all_to_all(view_out, TP, 0, 0)]
    all_gather x1 -> x0, waiting for transfers between devices: 51.3 us -> none  [local(): lax.all_gather(normed_rows, TP, axis=0, tiled=True)]
    all_to_all x0 -> x1, starting transfers between devices: none -> 11 us  [ports_arrange(): res = lax.all_to_all(view_out, TP, 0, 0)]
    another operation x0 -> x2, local copies, waits for them, and re-layouts: none -> 4.32 us  [ports_arrange(): view_out = jnp.stack(m_next)]
where the time goes in v1:
time: 417 us; the launch traced here: 416 us
  waiting for transfers between devices  119 us (29%)
  blocking collectives  101 us (24%)
  matrix products  88.1 us (21%)
  other arithmetic  47.7 us (11%)
  local copies, waits for them, and re-layouts  30.7 us (7%)
  starting transfers between devices  28.6 us (7%)
    all_to_all x1, waiting for transfers between devices, ports_arrange(): res = lax.all_to_all(view_out, TP, 0, 0)  93.6 us
    all_gather x4, blocking collectives, gathered_once(): both, at, found = (lax.all_gather(jnp.concatenate(lines), axis), 0, {})  38.2 us
    dot_general x4, matrix products, advance(): jnp.dot(query_rows, block_pair[0].T, preferred_element_type=jnp.float32)  37.5 us
    reduce_sum x5, other arithmetic, fold_block(): row_sum = row_sum * fading + jnp.sum(weights, axis=1)  34.2 us
    dot_general x5, matrix products, fold_block(): jnp.dot(weights.astype(jnp.bfloat16), value_rows, preferred_element_type=...  32.5 us
    all_to_all x2, blocking collectives, sent_to_all(): lax.all_to_all(jnp.broadcast_to(value[None], (count, *value.shape)), axis...  31.2 us
    all_to_all x1, blocking collectives, sent_together(): lax.all_to_all(both, axis, split_axis=split_dim, concat_axis=concat_dim,...  18.9 us
    all_to_all x1, waiting for transfers between devices, sent_to_all(): lax.all_to_all(jnp.broadcast_to(value[None], (count, *value.shape)), axis...  15.7 us
  transfers between devices with their start and end apart: 3, of which 3 were waited for; matrix products, arithmetic and copies ran while one was open for 0% of the time, Pallas kernels for 0%

profile of v1, /device:TPU:1, one launch (start us, length us, event | category | flops | bytes accessed | tf_op | source)
XLA Modules:
  0.0 416.3 jit_solution(2352424080007007937)
XLA Ops:
  0.6 0.0 copy-start
  0.6 2.1 broadcast_in_dim.24
  2.7 8.5 %all-to-all-start = ((bf16[16,32,1024]{2,1,0:T(8,128)(2,1)}), bf16[16,32,1024]{2,1,0:T(8,128)(2,1)}, u32[]{:S(2)}, u32[]{:S(2)}) async-start(bf16[16,32,1024]{2,1,0:T(8,128)(2,1)} %broadcast_in_dim.24), calls=%async_computation | async-start | bytes 2097152 | tf_op jit(solution)/shard_map/all_to_all | solution.py:26
  11.3 15.7 %all-to-all-done = bf16[16,32,1024]{2,1,0:T(8,128)(2,1)} async-done(((bf16[16,32,1024]{2,1,0:T(8,128)(2,1)}), bf16[16,32,1024]{2,1,0:T(8,128)(2,1)}, u32[]{:S(2)}, u32[]{:S(2)}) %all-to-all-start) | async-done | bytes 1048608 | tf_op jit(solution)/shard_map/all_to_all | solution.py:26
  26.9 1.5 copy.25
  28.4 1.2 copy.19
  29.6 102.5 %while.15 = (s32[]{:T(128)}, f32[4096]{0:T(1024)S(1)}, f32[4096]{0:T(1024)S(1)}, f32[4096,128]{1,0:T(8,128)S(1)}, bf16[4,1024,128]{2,1,0:T(8,128)(2,1)}, /*index...) while((s32[]{:T(128)}, f32[4096]{0:T(1024)S(1)}, ...), condition=%wide.region_3.4_spmd.clone, body=%wide.region_0.3_spmd.clone.sunk | while | flops 2182631424 | bytes 56361076 | solution.py:125
  29.6 9.4 %multiply_reduce_fusion.5 = (f32[4096]{0:T(1024)S(1)}, f32[1024,4096]{1,0:T(8,128)}) fusion(bf16[4096,128]{1,0:T(8,128)(2,1)} %get-tuple-element.183, bf16[4,1024,128]{2,1,0:T(8,128)(2,1)} %get-tuple-element.182, s32[]{:T(128)S(6)} %copy.32), kind=kOutput, calls=%fused_computation.1.clone.1 | convolution fusion | flops 1082126336 | bytes 18104324 | tf_op jit(solution)/shard_map/while/body/eval_jaxpr/dot_general | solution.py:117
  39.0 8.5 %fusion.99 = f32[4096]{0:T(1024)S(1)} fusion(f32[1024,4096]{1,0:T(8,128)} %get-tuple-element.157, f32[4096]{0:T(1024)S(1)} %select_maximum_fusion.2), kind=kLoop, calls=%fused_computation.3.clone.1 | loop fusion | flops 12578816 | bytes 16809984 | tf_op jit(solution)/shard_map/while/body/eval_jaxpr/reduce_sum | solution.py:99
  47.5 7.7 %fusion.101 = f32[4096,128]{1,0:T(8,128)S(1)} fusion(f32[1024,4096]{1,0:T(8,128)} %get-tuple-element.157, f32[4096]{0:T(1024)S(1)} %select_maximum_fusion.2, f32[4096,128]{1,0:T(8,128)S(1)} %get-tuple-element.172, f32[4096]{0:T(1024)S(1)} %get-tuple-element.159, pred[]{:T(512)S(6)} %compare.4, bf16[4,1024,128]{2,1,0:T(8,128)(2,1)} %get-tuple-element.184, ...), kind=kOutput, calls=%fused_computation.7.clone.1 | convolution fusion | flops 1087897600 | bytes 21266436 | tf_op jit(solution)/shard_map/while/body/eval_jaxpr/dot_general | solution.py:100
  55.2 9.4 %multiply_reduce_fusion.5 = (f32[4096]{0:T(1024)S(1)}, f32[1024,4096]{1,0:T(8,128)}) fusion(bf16[4096,128]{1,0:T(8,128)(2,1)} %get-tuple-element.183, bf16[4,1024,128]{2,1,0:T(8,128)(2,1)} %get-tuple-element.182, s32[]{:T(128)S(6)} %copy.32), kind=kOutput, calls=%fused_computation.1.clone.1 | convolution fusion | flops 1082126336 | bytes 18104324 | tf_op jit(solution)/shard_map/while/body/eval_jaxpr/dot_general | solution.py:117
  64.6 8.5 %fusion.99 = f32[4096]{0:T(1024)S(1)} fusion(f32[1024,4096]{1,0:T(8,128)} %get-tuple-element.157, f32[4096]{0:T(1024)S(1)} %select_maximum_fusion.2), kind=kLoop, calls=%fused_computation.3.clone.1 | loop fusion | flops 12578816 | bytes 16809984 | tf_op jit(solution)/shard_map/while/body/eval_jaxpr/reduce_sum | solution.py:99
  73.2 7.7 %fusion.101 = f32[4096,128]{1,0:T(8,128)S(1)} fusion(f32[1024,4096]{1,0:T(8,128)} %get-tuple-element.157, f32[4096]{0:T(1024)S(1)} %select_maximum_fusion.2, f32[4096,128]{1,0:T(8,128)S(1)} %get-tuple-element.172, f32[4096]{0:T(1024)S(1)} %get-tuple-element.159, pred[]{:T(512)S(6)} %compare.4, bf16[4,1024,128]{2,1,0:T(8,128)(2,1)} %get-tuple-element.184, ...), kind=kOutput, calls=%fused_computation.7.clone.1 | convolution fusion | flops 1087897600 | bytes 21266436 | tf_op jit(solution)/shard_map/while/body/eval_jaxpr/dot_general | solution.py:100
  80.9 9.4 %multiply_reduce_fusion.5 = (f32[4096]{0:T(1024)S(1)}, f32[1024,4096]{1,0:T(8,128)}) fusion(bf16[4096,128]{1,0:T(8,128)(2,1)} %get-tuple-element.183, bf16[4,1024,128]{2,1,0:T(8,128)(2,1)} %get-tuple-element.182, s32[]{:T(128)S(6)} %copy.32), kind=kOutput, calls=%fused_computation.1.clone.1 | convolution fusion | flops 1082126336 | bytes 18104324 | tf_op jit(solution)/shard_map/while/body/eval_jaxpr/dot_general | solution.py:117
  90.2 8.5 %fusion.99 = f32[4096]{0:T(1024)S(1)} fusion(f32[1024,4096]{1,0:T(8,128)} %get-tuple-element.157, f32[4096]{0:T(1024)S(1)} %select_maximum_fusion.2), kind=kLoop, calls=%fused_computation.3.clone.1 | loop fusion | flops 12578816 | bytes 16809984 | tf_op jit(solution)/shard_map/while/body/eval_jaxpr/reduce_sum | solution.py:99
  98.8 7.7 %fusion.101 = f32[4096,128]{1,0:T(8,128)S(1)} fusion(f32[1024,4096]{1,0:T(8,128)} %get-tuple-element.157, f32[4096]{0:T(1024)S(1)} %select_maximum_fusion.2, f32[4096,128]{1,0:T(8,128)S(1)} %get-tuple-element.172, f32[4096]{0:T(1024)S(1)} %get-tuple-element.159, pred[]{:T(512)S(6)} %compare.4, bf16[4,1024,128]{2,1,0:T(8,128)(2,1)} %get-tuple-element.184, ...), kind=kOutput, calls=%fused_computation.7.clone.1 | convolution fusion | flops 1087897600 | bytes 21266436 | tf_op jit(solution)/shard_map/while/body/eval_jaxpr/dot_general | solution.py:100
  106.5 9.4 %multiply_reduce_fusion.5 = (f32[4096]{0:T(1024)S(1)}, f32[1024,4096]{1,0:T(8,128)}) fusion(bf16[4096,128]{1,0:T(8,128)(2,1)} %get-tuple-element.183, bf16[4,1024,128]{2,1,0:T(8,128)(2,1)} %get-tuple-element.182, s32[]{:T(128)S(6)} %copy.32), kind=kOutput, calls=%fused_computation.1.clone.1 | convolution fusion | flops 1082126336 | bytes 18104324 | tf_op jit(solution)/shard_map/while/body/eval_jaxpr/dot_general | solution.py:117
  115.9 8.5 %fusion.99 = f32[4096]{0:T(1024)S(1)} fusion(f32[1024,4096]{1,0:T(8,128)} %get-tuple-element.157, f32[4096]{0:T(1024)S(1)} %select_maximum_fusion.2), kind=kLoop, calls=%fused_computation.3.clone.1 | loop fusion | flops 12578816 | bytes 16809984 | tf_op jit(solution)/shard_map/while/body/eval_jaxpr/reduce_sum | solution.py:99
  124.4 7.7 %fusion.101 = f32[4096,128]{1,0:T(8,128)S(1)} fusion(f32[1024,4096]{1,0:T(8,128)} %get-tuple-element.157, f32[4096]{0:T(1024)S(1)} %select_maximum_fusion.2, f32[4096,128]{1,0:T(8,128)S(1)} %get-tuple-element.172, f32[4096]{0:T(1024)S(1)} %get-tuple-element.159, pred[]{:T(512)S(6)} %compare.4, bf16[4,1024,128]{2,1,0:T(8,128)(2,1)} %get-tuple-element.184, ...), kind=kOutput, calls=%fused_computation.7.clone.1 | convolution fusion | flops 1087897600 | bytes 21266436 | tf_op jit(solution)/shard_map/while/body/eval_jaxpr/dot_general | solution.py:100
  132.1 0.0 copy-start.4
  132.1 1.7 fusion.79
  133.9 0.1 fusion.22
  134.0 0.0 copy-done.4
  134.0 1.8 fusion.18
  135.8 1.5 copy.20
  137.4 1.1 pad_maximum_fusion
  138.4 5.2 %copy.21 = bf16[1,512,1040]{2,0,1:T(2,128)(2,1)S(1)} copy(bf16[1,512,1040]{1,2,0:T(8,128)(2,1)} %pad_maximum_fusion) | data formatting | bytes 2129920 | tf_op jit(solution)/shard_map/concatenate | solution.py:40
  143.7 0.5 broadcast.83
  144.2 9.2 %reduce.4 = bf16[512,1040]{1,0:T(8,128)(2,1)} reduce(bf16[512,1,1040]{2,1,0:T(2,128)(2,1)S(1)} %bitcast.307, bf16[]{:T(256)} %broadcast.83), dimensions={1}, to_apply=%bitcast.274.reduce_sub_computation | reduce | bytes 2129922
  153.4 3.9 reshape.903
  157.3 18.9 %all_to_all.37 = bf16[16,2,16640]{2,1,0:T(2,128)(2,1)} all-to-all(bf16[16,2,16640]{2,1,0:T(2,128)(2,1)S(1)} %reshape.903), channel_id=1, replica_groups=mesh['ctx_0'=4,'ctx_1'=4,'tp_0'=4,'tp_1'=2] {'ctx_0','ctx_1'}, dimensions={0} | all-to-all | bytes 2129920 | tf_op jit(solution)/shard_map/all_to_all | solution.py:43
  176.2 4.8 %reshape.904 = bf16[512,1,1040]{2,1,0:T(2,128)(2,1)S(1)} reshape(bf16[16,2,16640]{2,1,0:T(2,128)(2,1)} %all_to_all.37) | data formatting | bytes 2129920
  181.0 0.2 copy.23
  181.2 0.1 multiply_reduce_fusion.2
  181.4 0.9 copy-done.1
  182.2 2.0 mul.276
  184.2 1.7 mul.277
  185.9 1.8 multiply_reduce_fusion.1
  187.7 0.1 div.24
  187.8 0.1 broadcast_in_dim.26
  188.0 16.1 %all_to_all.38 = bf16[16,32,1024]{2,1,0:T(8,128)(2,1)S(1)} all-to-all(bf16[16,32,1024]{2,1,0:T(8,128)(2,1)S(1)} %broadcast_in_dim.26), channel_id=1, replica_groups=mesh['ctx_0'=4,'ctx_1'=4,'tp_0'=4,'tp_1'=2] {'ctx_0','ctx_1'}, dimensions={0} | all-to-all | bytes 2097152 | tf_op jit(solution)/shard_map/all_to_all | solution.py:26
  204.1 1.5 convolution_convert_fusion
  205.6 9.2 %all-to-all-start.3 = ((bf16[8,64,512]{2,1,0:T(8,128)(2,1)}), bf16[8,64,512]{2,1,0:T(8,128)(2,1)S(1)}, u32[]{:S(2)}, u32[]{:S(2)}) async-start(bf16[8,64,512]{2,1,0:T(8,128)(2,1)} %bitcast.12), calls=%async_computation.3 | async-start | bytes 1048576 | tf_op jit(solution)/shard_map/all_to_all | solution.py:58
  214.8 9.3 %all-to-all-done.3 = bf16[8,64,512]{2,1,0:T(8,128)(2,1)S(1)} async-done(((bf16[8,64,512]{2,1,0:T(8,128)(2,1)}), bf16[8,64,512]{2,1,0:T(8,128)(2,1)S(1)}, u32[]{:S(2)}, u32[]{:S(2)}) %all-to-all-start.3) | async-done | bytes 524320 | tf_op jit(solution)/shard_map/all_to_all | solution.py:58
  224.1 0.1 convert_reduce_fusion
  224.2 0.1 multiply_reduce_fusion.3
  224.3 6.8 %psum.14 = f32[64]{0:T(128)S(1)} all-reduce(f32[64]{0:T(128)S(1)} %multiply_reduce_fusion.3), channel_id=1, replica_groups=mesh['ctx_0'=4,'ctx_1'=4,'tp_0'=4,'tp_1'=2] {'ctx_0'}, use_global_device_ids=true, to_apply=%region_11.12 | all-reduce | flops 64 | bytes 512 | tf_op jit(solution)/shard_map/psum | solution.py:64
  231.1 6.3 %psum.15 = f32[64]{0:T(128)S(1)} all-reduce(f32[64]{0:T(128)S(1)} %psum.14), channel_id=1, replica_groups=mesh['ctx_0'=4,'ctx_1'=4,'tp_0'=4,'tp_1'=2] {'ctx_1'}, use_global_device_ids=true, to_apply=%region_12.13 | all-reduce | flops 64 | bytes 512 | tf_op jit(solution)/shard_map/psum | solution.py:64
  237.5 0.1 multiply_convert_fusion
  237.6 0.1 broadcast_in_dim.27
  237.7 15.1 %all_to_all.39 = bf16[16,64,512]{2,1,0:T(8,128)(2,1)S(1)} all-to-all(bf16[16,64,512]{2,1,0:T(8,128)(2,1)S(1)} %broadcast_in_dim.27), channel_id=1, replica_groups=mesh['ctx_0'=4,'ctx_1'=4,'tp_0'=4,'tp_1'=2] {'ctx_0','ctx_1'}, dimensions={0} | all-to-all | bytes 2097152 | tf_op jit(solution)/shard_map/all_to_all | solution.py:26
  252.7 0.1 copy.24
  252.8 4.2 %stack.3 = bf16[8,64,8192]{2,1,0:T(8,128)(2,1)} broadcast(bf16[64,8192]{1,0:T(8,128)(2,1)S(1)} %bitcast.312), dimensions={1,2} | broadcast | bytes 9437184 | tf_op jit(solution)/shard_map/stack | solution.py:231
  257.1 11.0 %all-to-all-start.5 = ((bf16[8,64,8192]{2,1,0:T(8,128)(2,1)}), bf16[8,64,8192]{2,1,0:T(8,128)(2,1)}, u32[]{:S(2)}, u32[]{:S(2)}) async-start(bf16[8,64,8192]{2,1,0:T(8,128)(2,1)} %stack.3), calls=%async_computation.5 | async-start | bytes 16777216 | tf_op jit(solution)/shard_map/all_to_all | solution.py:232
  268.1 0.2 reduce-window.8
  268.3 93.6 %all-to-all-done.5 = bf16[8,64,8192]{2,1,0:T(8,128)(2,1)} async-done(((bf16[8,64,8192]{2,1,0:T(8,128)(2,1)}), bf16[8,64,8192]{2,1,0:T(8,128)(2,1)}, u32[]{:S(2)}, u32[]{:S(2)}) %all-to-all-start.5) | async-done | bytes 8388640 | tf_op jit(solution)/shard_map/all_to_all | solution.py:232
  361.8 14.2 %fusion.80 = (f32[512]{0:T(512)S(1)}, f32[512,1002]{0,1:T(8,128)S(1)}) fusion(bf16[512,8192]{1,0:T(8,128)(2,1)} %bitcast.14, bf16[8192,1002]{0,1:T(8,128)(2,1)} %param.21), kind=kOutput, calls=%fused_computation.145 | convolution fusion | flops 8405897728 | bytes 26859520 | tf_op jit(solution)/shard_map/dot_general | solution.py:235
  376.1 0.5 exponential_reduce_fusion
  376.6 9.0 %all-gather.4 = f32[4,3,512]{2,1,0:T(4,128)S(1)} all-gather(f32[1,3,512]{2,1,0:T(4,128)S(1)} %maximum_bitcast_fusion), channel_id=2, replica_groups=mesh['ctx_0'=4,'ctx_1'=4,'tp_0'=4,'tp_1'=2] {'ctx_0'}, dimensions={0}, use_global_device_ids=true | all-gather | bytes 30720 | tf_op jit(solution)/shard_map/all_gather | solution.py:76
  385.7 9.0 %all-gather.5 = f32[4,3,512]{2,1,0:T(4,128)S(1)} all-gather(f32[1,3,512]{2,1,0:T(4,128)S(1)} %maximum_bitcast_fusion.1), channel_id=3, replica_groups=mesh['ctx_0'=4,'ctx_1'=4,'tp_0'=4,'tp_1'=2] {'ctx_1'}, dimensions={0}, use_global_device_ids=true | all-gather | bytes 30720 | tf_op jit(solution)/shard_map/all_gather | solution.py:76
  394.8 9.0 %all-gather.6 = f32[4,3,512]{2,1,0:T(4,128)S(1)} all-gather(f32[1,3,512]{2,1,0:T(4,128)S(1)} %maximum_bitcast_fusion.2), channel_id=4, replica_groups=mesh['ctx_0'=4,'ctx_1'=4,'tp_0'=4,'tp_1'=2] {'tp_0'}, dimensions={0}, use_global_device_ids=true | all-gather | bytes 30720 | tf_op jit(solution)/shard_map/all_gather | solution.py:76
  403.9 11.1 %all-gather.7 = f32[2,3,512]{2,1,0:T(4,128)S(1)} all-gather(f32[1,3,512]{2,1,0:T(4,128)S(1)} %maximum_bitcast_fusion.3), channel_id=5, replica_groups=mesh['ctx_0'=4,'ctx_1'=4,'tp_0'=4,'tp_1'=2] {'tp_1'}, dimensions={0}, use_global_device_ids=true | all-gather | bytes 18432 | tf_op jit(solution)/shard_map/all_gather | solution.py:76
  415.0 0.6 dynamic_slice.10
  415.6 0.7 fusion.20
  (52 shorter events, 0.5 us)
Async XLA Ops:
  0.6 203.5 %copy-start = (bf16[1024,512]{1,0:T(8,128)(2,1)S(1)}, bf16[1024,512]{1,0:T(8,128)(2,1)}, u32[]{:S(2)}) copy-start(bf16[1024,512]{1,0:T(8,128)(2,1)} %param.18) | copy-start | bytes 3145732
  2.7 24.2 %all-to-all-start = ((bf16[16,32,1024]{2,1,0:T(8,128)(2,1)}), bf16[16,32,1024]{2,1,0:T(8,128)(2,1)}, u32[]{:S(2)}, u32[]{:S(2)}) async-start(bf16[16,32,1024]{2,1,0:T(8,128)(2,1)} %broadcast_in_dim.24), calls=%async_computation | async-start | bytes 2097152 | tf_op jit(solution)/shard_map/all_to_all | solution.py:26
  29.6 102.5 %copy-start.3 = (bf16[32,128]{1,0:T(8,128)(2,1)S(1)}, bf16[32,128]{1,0:T(8,128)(2,1)}, u32[]{:S(2)}) copy-start(bf16[32,128]{1,0:T(8,128)(2,1)} %param.16) | copy-start | bytes 24580
  132.1 1.9 copy-start.4
  181.2 1.0 copy-start.1
  204.1 10.7 %copy-start.6 = (bf16[512]{0:T(512)(128)(2,1)S(1)}, bf16[512]{0:T(512)(128)(2,1)}, u32[]{:S(2)}) copy-start(bf16[512]{0:T(512)(128)(2,1)} %param.20) | copy-start | bytes 3076
  204.1 20.1 %copy-start.2 = (bf16[64,512]{1,0:T(8,128)(2,1)S(1)}, bf16[64,512]{1,0:T(8,128)(2,1)}, u32[]{:S(2)}) copy-start(bf16[64,512]{1,0:T(8,128)(2,1)} %param.19) | copy-start | bytes 196612
  205.6 18.5 %all-to-all-start.3 = ((bf16[8,64,512]{2,1,0:T(8,128)(2,1)}), bf16[8,64,512]{2,1,0:T(8,128)(2,1)S(1)}, u32[]{:S(2)}, u32[]{:S(2)}) async-start(bf16[8,64,512]{2,1,0:T(8,128)(2,1)} %bitcast.12), calls=%async_computation.3 | async-start | bytes 1048576 | tf_op jit(solution)/shard_map/all_to_all | solution.py:58
  257.1 11.0 %copy-start.7 = (s32[8]{0:T(128)S(1)}, s32[8]{0:T(128)}, u32[]{:S(2)}) copy-start(s32[8]{0:T(128)} %param.23) | copy-start | bytes 100
  257.1 104.8 %all-to-all-start.5 = ((bf16[8,64,8192]{2,1,0:T(8,128)(2,1)}), bf16[8,64,8192]{2,1,0:T(8,128)(2,1)}, u32[]{:S(2)}, u32[]{:S(2)}) async-start(bf16[8,64,8192]{2,1,0:T(8,128)(2,1)} %stack.3), calls=%async_computation.5 | async-start | bytes 16777216 | tf_op jit(solution)/shard_map/all_to_all | solution.py:232
  361.8 14.2 %copy-start.5 = (s32[512]{0:T(512)S(1)}, s32[512]{0:T(512)}, u32[]{:S(2)}) copy-start(s32[512]{0:T(512)} %param.22) | copy-start | bytes 6148
